TPU v7x, 256 devices: a whole 4x4x8 slice. The times are simulated.
256 devices in a mesh: obs: 64 (over z, y, core), rep: 4 (over x).
Axes of the slice: x: 4, y: 4, z: 8, core: 2. Of those that a mesh axis runs over, the one named last changes fastest.
Arguments:
- jacobians: float32 [18, 8388608], P(None, ('obs', 'rep')), may hold values from -3 to 3
- residuals: float32 [2, 8388608], P(None, ('obs', 'rep')), may hold values from -6 to 6
- camera_local: int32 [8388608], P(('obs', 'rep')), may hold values from 0 to 1023
- bucket_counts: int32 [256, 64], P(('obs', 'rep')), may hold values from 1 to 512, as said below
- camera_map: int32 [65536], replicated, may hold values from 0 to 65535, each once
Outputs:
- gradient: float32 [9, 65536], replicated
- camera_blocks: float32 [81, 65536], P(None, 'obs')
Inputs may be any that keep to these rules, and one draw needn't show every extreme that they name: bucket_counts[s, d] counts the leading live slots of bucket d of source block s; exactly one destination d has all 512 slots live from every source block, and every other bucket has at most 256 live slots. A slot in bucket d names camera slot d * 1024 + camera_local. `camera_map`: each camera id appears once.
All inputs are finite; a program needn't handle non-finite values.
Results may differ from a plain program's by a relative error of at most 0.0003.
Values sent between devices are 32-bit elements; how exact they have to be, the bound alone decides.
A program may use at most 192 MiB of HBM per device.

v0:
```python
import math
import jax
import jax.numpy as jnp
from jax import lax
from jax.sharding import Mesh
from jax.sharding import PartitionSpec as P

CAM_DEV = 1024
OBS = ("obs_0", "obs_1", "obs_2")
OBS_REP = ("obs_0", "obs_1", "obs_2", "rep")


def sent_together(arrays, axis, split_dim, concat_dim, along):
    widths = [a.shape[along] for a in arrays]
    both = jnp.concatenate(arrays, axis=along)
    filled = lax.all_to_all(both, axis, split_axis=split_dim, concat_axis=concat_dim, tiled=True)
    return tuple(jnp.split(filled, [sum(widths[:k]) for k in range(1, len(widths))], axis=along))


def split_up(shard, dim, count):
    shape = shard.shape
    pieces = shard.reshape(*shape[:dim], count, shape[dim] // count, *shape[dim + 1 :])
    return jnp.moveaxis(pieces, dim, 0)


def summed_on_arrival(shard, axis, dim):
    pieces = split_up(shard, dim, lax.axis_size(axis))
    arrived = lax.all_to_all(pieces, axis, split_axis=0, concat_axis=0, tiled=True)
    return arrived.sum(axis=0)


def side_by_side(arrays, axis, dim, along):
    both = jnp.concatenate(arrays, axis=along)
    filled, at, finished = (summed_on_arrival(both, axis, dim), 0, [])
    for a in arrays:
        finished.append(lax.slice_in_dim(filled, at, at + a.shape[along], axis=along))
        at += a.shape[along]
    return tuple(finished)


def in_order(pieces, dim):
    shape = list(pieces.shape[1:])
    shape[dim] *= pieces.shape[0]
    return jnp.moveaxis(pieces, 0, dim).reshape(shape)


def stacked_from(shard, axes, order):
    pieces = shard[None]
    for k in order:
        pieces = lax.all_gather(pieces, axes[k], axis=0, tiled=True)
    carried = [lax.axis_size(axes[k]) for k in reversed(order)]
    pieces = pieces.reshape(*carried, *shard.shape)
    turned = sorted(range(len(order)), key=lambda place: order[len(order) - 1 - place])
    return pieces.transpose(*turned, *range(len(order), pieces.ndim)).reshape(-1, *shard.shape)


def whole_of(shard, axes, order, dim):
    return in_order(stacked_from(shard, axes, order), dim)


def sent_to_all(shard, axis):
    count = lax.axis_size(axis)
    return lax.all_to_all(
        jnp.broadcast_to(shard[None], (count, *shard.shape)), axis, 0, 0, tiled=True
    )


def gather_directly(shard, axis, dim):
    return in_order(sent_to_all(shard, axis), dim)


def observation_terms(jacobs, resids):
    leading_row = jacobs[0:9]
    trailing_row = jacobs[9:18]
    gradient_terms = leading_row * resids[0:1] + trailing_row * resids[1:2]
    block_terms = (
        leading_row[:, None] * leading_row[None, :] + trailing_row[:, None] * trailing_row[None, :]
    )
    block_terms = block_terms.reshape((81,) + leading_row.shape[1:])
    return jnp.concatenate([gradient_terms, block_terms], axis=0)


def grouped_sums(jac_flat, res_flat, ids_flat, live_flat, width):
    total = jac_flat.shape[1]
    groups = total // width
    camera_rows = lax.broadcasted_iota(jnp.int32, (CAM_DEV, 1), 0)

    def add_group(index, summed):
        start = index * width
        jac_piece = lax.dynamic_slice_in_dim(jac_flat, start, width, 1)
        res_piece = lax.dynamic_slice_in_dim(res_flat, start, width, 1)
        id_piece = lax.dynamic_slice_in_dim(ids_flat, start, width, 0)
        live_piece = lax.dynamic_slice_in_dim(live_flat, start, width, 0)[None, :]
        terms = observation_terms(jac_piece * live_piece, res_piece * live_piece)
        one_hot = (id_piece[None, :] == camera_rows).astype(jnp.float32)
        added = lax.dot_general(
            terms,
            one_hot,
            (((1,), (1,)), ((), ())),
            precision=lax.Precision.HIGHEST,
            preferred_element_type=jnp.float32,
        )
        return summed + added

    return lax.fori_loop(0, groups, add_group, jnp.zeros((90, CAM_DEV), jnp.float32))


def group_width(senders, width):
    return math.gcd(senders, max(1, 2048 // width)) * width


def local(jacobians, residuals, camera_local, bucket_counts, camera_map):
    senders = lax.axis_size(OBS)
    capacity = jacobians.shape[1] // senders
    jac_split = jacobians.reshape(18, senders, capacity)
    res_split = residuals.reshape(2, senders, capacity)
    ids_split = camera_local.reshape(1, senders, capacity)
    counts_here = bucket_counts.reshape(1, senders, 1)
    moved_jac, moved_res = sent_together((jac_split, res_split), OBS, 1, 1, 0)
    moved_ids, moved_counts = sent_together((ids_split, counts_here), OBS, 1, 1, 2)
    within = lax.broadcasted_iota(jnp.int32, (1, senders, capacity), 2)
    live_mask = (within < moved_counts).astype(jnp.float32)
    summed = grouped_sums(
        moved_jac.reshape(18, senders * capacity),
        moved_res.reshape(2, senders * capacity),
        moved_ids.reshape(senders * capacity),
        live_mask.reshape(senders * capacity),
        group_width(senders, capacity),
    )
    grad_part = summed[:9]
    block_part = summed[9:]
    grad_share, block_share = side_by_side((grad_part, block_part), "rep", 1, 0)
    grad_slots = whole_of(grad_share, OBS_REP, (0, 1, 3, 2), 1)
    blocks_out = gather_directly(block_share, "rep", 1)
    gradient = (
        jnp.zeros(grad_slots.shape, jnp.float32)
        .at[:, camera_map]
        .set(grad_slots, unique_indices=True)
    )
    return (gradient, blocks_out)


def solution(mesh):
    split = Mesh(
        mesh.devices.reshape(8, 4, 2, mesh.shape["rep"]), ("obs_0", "obs_1", "obs_2", "rep")
    )
    return jax.shard_map(
        local,
        mesh=split,
        in_specs=(P(None, OBS_REP), P(None, OBS_REP), P(OBS_REP), P(OBS_REP, None), P()),
        out_specs=(P(), P(None, OBS)),
        check_vma=False,
    )
```

profile of v0, /device:TPU:1, one launch (start us, length us, event | category | flops | bytes accessed | tf_op | source)
XLA Modules:
  0.0 553.7 jit_solution(11730834584020948406)
XLA Ops:
  9.7 13.1 %all-to-all-start.1 = ((s32[1,64,513]{2,0,1:T(1,128)}), s32[1,64,513]{2,0,1:T(1,128)S(1)}, u32[]{:S(2)}, u32[]{:S(2)}) async-start(s32[1,64,513]{2,0,1:T(1,128)} %copy.22), calls=%async_computation.1 | async-start | bytes 327680 | tf_op jit(solution)/shard_map/all_to_all | solution.py:16
  34.5 6.9 %all-to-all-start = ((f32[20,64,512]{2,0,1:T(8,128)}), f32[20,64,512]{2,0,1:T(8,128)S(1)}, u32[]{:S(2)}, u32[]{:S(2)}) async-start(f32[20,64,512]{2,0,1:T(8,128)} %copy.19), calls=%async_computation | async-start | bytes 6291456 | tf_op jit(solution)/shard_map/all_to_all | solution.py:16
  43.8 70.0 %all-to-all-done = f32[20,64,512]{2,0,1:T(8,128)S(1)} async-done(((f32[20,64,512]{2,0,1:T(8,128)}), f32[20,64,512]{2,0,1:T(8,128)S(1)}, u32[]{:S(2)}, u32[]{:S(2)}) %all-to-all-start) | async-done | bytes 2621472 | tf_op jit(solution)/shard_map/all_to_all | solution.py:16
  119.3 118.1 %while.14 = (s32[]{:T(128)}, f32[90,1024]{1,0:T(8,128)}, f32[18,32768]{1,0:T(8,128)}, f32[32768]{0:T(1024)}, f32[2,32768]{1,0:T(2,128)S(1)}, /*index=5*/s32[3276...) while((s32[]{:T(128)}, f32[90,1024]{1,0:T(8,128)}, f32[18,32768]{1,0:T(8,128)}, ...), condition=%wide.region_1.0_spmd.clone, body=%wide.region_0.0_spmd.clone.sunk | while | flops 2267983872 | bytes 7364837 | solution.py:105
  121.4 4.6 fusion.17
  128.8 4.6 fusion.17
  136.1 4.6 fusion.17
  143.5 4.6 fusion.17
  150.9 4.6 fusion.17
  158.3 4.6 fusion.17
  165.6 4.6 fusion.17
  173.0 4.6 fusion.17
  209.9 4.6 fusion.17
  217.3 4.6 fusion.17
  238.6 10.0 %all_to_all.20 = f32[4,90,256]{2,1,0:T(8,128)S(1)} all-to-all(f32[4,90,256]{2,1,0:T(8,128)S(1)} %copy.23), channel_id=1, replica_groups=mesh['obs_0'=8,'obs_1'=4,'obs_2'=2,'rep'=4] {'rep'}, dimensions={0} | all-to-all | bytes 737280 | tf_op jit(solution)/shard_map/all_to_all | solution.py:28
  248.7 21.8 %all-gather.1 = f32[8,9,256]{2,1,0:T(8,128)S(1)} all-gather(f32[1,9,256]{2,1,0:T(8,128)S(1)} %slice_bitcast_fusion), channel_id=2, replica_groups=mesh['obs_0'=8,'obs_1'=4,'obs_2'=2,'rep'=4] {'obs_0'}, dimensions={0}, use_global_device_ids=true | all-gather | bytes 82944 | tf_op jit(solution)/shard_map/all_gather | solution.py:50
  270.6 10.2 %all_gather.13 = f32[32,9,256]{2,0,1:T(8,128)} all-gather(f32[8,9,256]{2,0,1:T(8,128)S(1)} %copy.24), channel_id=1, replica_groups=mesh['obs_0'=8,'obs_1'=4,'obs_2'=2,'rep'=4] {'obs_1'}, dimensions={0}, use_global_device_ids=true | all-gather | bytes 368640 | tf_op jit(solution)/shard_map/all_gather | solution.py:50
  280.8 28.4 %all-gather.5.cloned.1.call-done = f32[128,9,256]{2,0,1:T(8,128)} async-done(((f32[32,9,256]{2,0,1:T(8,128)}), f32[128,9,256]{2,0,1:T(8,128)}) %all-gather.5.cloned.1.call-update) | async-done | bytes 1179664 | tf_op jit(solution)/shard_map/all_gather | solution.py:50
  313.7 6.0 %all-to-all-done.3 = f32[4,81,256]{2,1,0:T(8,128)S(1)} async-done(((f32[4,81,256]{2,1,0:T(8,128)}), f32[4,81,256]{2,1,0:T(8,128)S(1)}, u32[]{:S(2)}, u32[]{:S(2)}) %all-to-all-start.3) | async-done | bytes 331808 | tf_op jit(solution)/shard_map/all_to_all | solution.py:63
  320.7 10.1 %all-gather.7.cloned.1.call-done = f32[256,9,256]{2,0,1:T(8,128)} async-done(((f32[128,9,256]{2,0,1:T(8,128)}), f32[256,9,256]{2,0,1:T(8,128)}) %all-gather.7.cloned.1.call-update) | async-done | bytes 2359312 | tf_op jit(solution)/shard_map/all_gather | solution.py:50
  330.8 4.6 copy.37
  338.1 16.6 %copy.29 = f32[9,256,256]{0,2,1:T(8,128)} copy(f32[9,256,256]{2,1,0:T(8,128)S(1)} %bitcast.45) | data formatting | bytes 4718592 | tf_op jit(solution)/shard_map/reshape | solution.py:44
  354.7 172.8 %scatter_custom_fusion = f32[9,65536]{0,1:T(8,128)} fusion(s32[65536]{0:T(1024)S(1)} %compare_select_fusion, f32[65536,9]{1,0:T(8,128)} %bitcast.41, f32[]{:T(128)} %constant.34.clone.1), kind=kCustom, calls=%fused_computation.14 | custom fusion | bytes 2359808 | tf_op jit(solution)/shard_map/scatter | solution.py:138
  527.5 19.4 %copy.28 = f32[9,65536]{1,0:T(8,128)} copy(f32[9,65536]{0,1:T(8,128)} %scatter_custom_fusion) | data formatting | bytes 4718592
  (243 shorter events, 102.7 us)
Async XLA Ops:
  9.7 24.8 %all-to-all-start.1 = ((s32[1,64,513]{2,0,1:T(1,128)}), s32[1,64,513]{2,0,1:T(1,128)S(1)}, u32[]{:S(2)}, u32[]{:S(2)}) async-start(s32[1,64,513]{2,0,1:T(1,128)} %copy.22), calls=%async_computation.1 | async-start | bytes 327680 | tf_op jit(solution)/shard_map/all_to_all | solution.py:16
  34.5 7.2 %copy-start = (s32[1,64,513]{2,0,1:T(1,128)}, s32[1,64,513]{2,0,1:T(1,128)S(1)}, u32[]{:S(2)}) copy-start(s32[1,64,513]{2,0,1:T(1,128)S(1)} %all-to-all-done.1) | copy-start | bytes 393988
  34.5 79.4 %all-to-all-start = ((f32[20,64,512]{2,0,1:T(8,128)}), f32[20,64,512]{2,0,1:T(8,128)S(1)}, u32[]{:S(2)}, u32[]{:S(2)}) async-start(f32[20,64,512]{2,0,1:T(8,128)} %copy.19), calls=%async_computation | async-start | bytes 6291456 | tf_op jit(solution)/shard_map/all_to_all | solution.py:16
  41.4 267.8 %all-gather.5.cloned.1.call-start = ((), (), s32[]{:S(2)}) async-start(), calls=%async_computation.4 | async-start | bytes 1474560 | tf_op jit(solution)/shard_map/all_gather | solution.py:50
  115.6 3.6 slice-start
  119.3 2.1 copy-start.1
  126.7 2.1 copy-start.1
  134.1 2.1 copy-start.1
  141.4 2.1 copy-start.1
  148.8 2.1 copy-start.1
  156.2 2.1 copy-start.1
  163.6 2.1 copy-start.1
  171.0 2.1 copy-start.1
  178.3 2.1 copy-start.1
  185.7 2.1 copy-start.1
  193.1 2.1 copy-start.1
  200.5 2.1 copy-start.1
  207.8 2.1 copy-start.1
  215.2 2.1 copy-start.1
  222.6 2.1 copy-start.1
  230.0 2.1 copy-start.1
  237.3 76.3 %copy-start.4 = (s32[65536]{0:T(1024)S(1)}, s32[65536]{0:T(1024)}, u32[]{:S(2)}) copy-start(s32[65536]{0:T(1024)} %param.11) | copy-start | bytes 786436
  280.8 50.0 %all-gather.7.cloned.1.call-start = ((), (), s32[]{:S(2)}) async-start(), calls=%async_computation.5 | async-start | bytes 3538944 | tf_op jit(solution)/shard_map/all_gather | solution.py:50
  310.0 9.7 %all-to-all-start.3 = ((f32[4,81,256]{2,1,0:T(8,128)}), f32[4,81,256]{2,1,0:T(8,128)S(1)}, u32[]{:S(2)}, u32[]{:S(2)}) async-start(f32[4,81,256]{2,1,0:T(8,128)} %broadcast_in_dim.40), calls=%async_computation.3 | async-start | bytes 720896 | tf_op jit(solution)/shard_map/all_to_all | solution.py:63
  (17 other events, 12.8 us)
Sparse Core Ops, SparseCore 0:
  280.9 28.2 all-gather.4
  311.0 19.7 all-gather.6
where the time goes:
time: 555 us; the launch traced here: 554 us
  local copies, waits for them, and re-layouts  262 us (47%)
  waiting for transfers between devices  118 us (21%)
  matrix products  72.9 us (13%)
  blocking collectives  42 us (8%)
  starting transfers between devices  24 us (4%)
  other arithmetic  19.5 us (4%)
  between operations  14.2 us (3%)
    scatter x1, local copies, waits for them, and re-layouts, local(): gradient = jnp.zeros(grad_slots.shape, jnp.float32).at[:, camera_map].set...  173 us
    all_to_all x2, waiting for transfers between devices, sent_together(): lax.all_to_all(both, axis, split_axis=split_dim, concat_axis=concat_dim,...  73.4 us
    dot_general x16, matrix products, add_group(): lax.dot_general(terms, one_hot, (((1,), (1,)), ((), ())), precision=lax.P...  72.9 us
    all_gather x2, waiting for transfers between devices, stacked_from(): pieces = lax.all_gather(pieces, axes[k], axis=0, tiled=True)  38.4 us
    all_gather x2, blocking collectives, stacked_from(): pieces = lax.all_gather(pieces, axes[k], axis=0, tiled=True)  32 us
    unnamed x16, local copies, waits for them, and re-layouts  28.7 us
    all_to_all x2, starting transfers between devices, sent_together(): lax.all_to_all(both, axis, split_axis=split_dim, concat_axis=concat_dim,...  20.1 us
    reshape x1, local copies, waits for them, and re-layouts, in_order(): return jnp.moveaxis(pieces, 0, dim).reshape(shape)  16.6 us
  transfers between devices with their start and end apart: 5, of which 5 were waited for; matrix products, arithmetic and copies ran while one was open for 2% of the time, Pallas kernels for 0%

commit v1 on v0

--- a/solution.py
+++ b/solution.py
@@ -8,6 +8,11 @@
 CAM_DEV = 1024
 OBS = ("obs_0", "obs_1", "obs_2")
 OBS_REP = ("obs_0", "obs_1", "obs_2", "rep")
+
+
+def all_by_exchange(x, axis, d):
+    sent = jnp.stack([x] * lax.axis_size(axis))
+    return jnp.concatenate(lax.all_to_all(sent, axis, 0, 0), axis=d)
 
 
 def sent_together(arrays, axis, split_dim, concat_dim, along):
@@ -47,7 +52,7 @@
 def stacked_from(shard, axes, order):
     pieces = shard[None]
     for k in order:
-        pieces = lax.all_gather(pieces, axes[k], axis=0, tiled=True)
+        pieces = all_by_exchange(pieces, axes[k], 0)
     carried = [lax.axis_size(axes[k]) for k in reversed(order)]
     pieces = pieces.reshape(*carried, *shard.shape)
     turned = sorted(range(len(order)), key=lambda place: order[len(order) - 1 - place])

time: 555 us -> 521 us (0.939)
  waiting for transfers between devices: 118 us -> 96.3 us
  between operations: 14.2 us -> 0.88 us
  blocking collectives: 42 us -> 35 us
  starting transfers between devices: 24 us -> 30.6 us
    all_gather x2 -> x0, waiting for transfers between devices: 38.4 us -> none  [stacked_from(): pieces = lax.all_gather(pieces, axes[k], axis=0, tiled=True)]
    all_gather x2 -> x0, blocking collectives: 32 us -> none  [stacked_from(): pieces = lax.all_gather(pieces, axes[k], axis=0, tiled=True)]
    all_to_all x0 -> x2, blocking collectives: none -> 24.9 us  [all_by_exchange(): return jnp.concatenate(lax.all_to_all(sent, axis, 0, 0), axis=d)]
    all_to_all x0 -> x2, waiting for transfers between devices: none -> 16.7 us  [all_by_exchange(): return jnp.concatenate(lax.all_to_all(sent, axis, 0, 0), axis=d)]
    all_to_all x0 -> x2, starting transfers between devices: none -> 6.98 us  [all_by_exchange(): return jnp.concatenate(lax.all_to_all(sent, axis, 0, 0), axis=d)]
    unnamed x16 -> x15, local copies, waits for them, and re-layouts: 28.7 us -> 28.7 us
where the time goes in v1:
time: 521 us; the launch traced here: 519 us
  local copies, waits for them, and re-layouts  262 us (50%)
  waiting for transfers between devices  96.3 us (18%)
  matrix products  72.9 us (14%)
  blocking collectives  35 us (7%)
  starting transfers between devices  30.6 us (6%)
  other arithmetic  19.8 us (4%)
    scatter x1, local copies, waits for them, and re-layouts, local(): gradient = jnp.zeros(grad_slots.shape, jnp.float32).at[:, camera_map].set...  173 us
    all_to_all x2, waiting for transfers between devices, sent_together(): lax.all_to_all(both, axis, split_axis=split_dim, concat_axis=concat_dim,...  73.6 us
    dot_general x16, matrix products, add_group(): lax.dot_general(terms, one_hot, (((1,), (1,)), ((), ())), precision=lax.P...  72.9 us
    unnamed x15, local copies, waits for them, and re-layouts  28.7 us
    all_to_all x2, blocking collectives, all_by_exchange(): return jnp.concatenate(lax.all_to_all(sent, axis, 0, 0), axis=d)  24.9 us
    all_to_all x2, starting transfers between devices, sent_together(): lax.all_to_all(both, axis, split_axis=split_dim, concat_axis=concat_dim,...  20.1 us
    reshape x1, local copies, waits for them, and re-layouts, in_order(): return jnp.moveaxis(pieces, 0, dim).reshape(shape)  16.8 us
    all_to_all x2, waiting for transfers between devices, all_by_exchange(): return jnp.concatenate(lax.all_to_all(sent, axis, 0, 0), axis=d)  16.7 us
  transfers between devices with their start and end apart: 5, of which 5 were waited for; matrix products, arithmetic and copies ran while one was open for 2% of the time, Pallas kernels for 0%

profile of v1, /device:TPU:1, one launch (start us, length us, event | category | flops | bytes accessed | tf_op | source)
XLA Modules:
  0.0 519.0 jit_solution(4445822576633463569)
XLA Ops:
  3.2 13.1 %all-to-all-start.1 = ((s32[1,64,513]{2,0,1:T(1,128)}), s32[1,64,513]{2,0,1:T(1,128)S(1)}, u32[]{:S(2)}, u32[]{:S(2)}) async-start(s32[1,64,513]{2,0,1:T(1,128)} %copy.48), calls=%async_computation.1 | async-start | bytes 327680 | tf_op jit(solution)/shard_map/all_to_all | solution.py:21
  28.0 6.9 %all-to-all-start = ((f32[20,64,512]{2,0,1:T(8,128)}), f32[20,64,512]{2,0,1:T(8,128)S(1)}, u32[]{:S(2)}, u32[]{:S(2)}) async-start(f32[20,64,512]{2,0,1:T(8,128)} %copy.45), calls=%async_computation | async-start | bytes 6291456 | tf_op jit(solution)/shard_map/all_to_all | solution.py:21
  37.1 70.3 %all-to-all-done = f32[20,64,512]{2,0,1:T(8,128)S(1)} async-done(((f32[20,64,512]{2,0,1:T(8,128)}), f32[20,64,512]{2,0,1:T(8,128)S(1)}, u32[]{:S(2)}, u32[]{:S(2)}) %all-to-all-start) | async-done | bytes 2621472 | tf_op jit(solution)/shard_map/all_to_all | solution.py:21
  112.8 118.1 %while.14 = (s32[]{:T(128)}, f32[90,1024]{1,0:T(8,128)}, f32[18,32768]{1,0:T(8,128)}, f32[32768]{0:T(1024)}, f32[2,32768]{1,0:T(2,128)S(1)}, /*index=5*/s32[3276...) while((s32[]{:T(128)}, f32[90,1024]{1,0:T(8,128)}, f32[18,32768]{1,0:T(8,128)}, ...), condition=%wide.region_1.0_spmd.clone, body=%wide.region_0.0_spmd.clone.sunk | while | flops 2267983872 | bytes 7364837 | solution.py:110
  114.9 4.6 fusion.17
  122.2 4.6 fusion.17
  129.6 4.6 fusion.17
  137.0 4.6 fusion.17
  144.4 4.6 fusion.17
  151.7 4.6 fusion.17
  159.1 4.6 fusion.17
  166.5 4.6 fusion.17
  173.9 4.6 fusion.17
  196.0 4.6 fusion.17
  203.4 4.6 fusion.17
  232.1 10.0 %all_to_all.40 = f32[4,90,256]{2,1,0:T(8,128)S(1)} all-to-all(f32[4,90,256]{2,1,0:T(8,128)S(1)} %copy.49), channel_id=1, replica_groups=mesh['obs_0'=8,'obs_1'=4,'obs_2'=2,'rep'=4] {'rep'}, dimensions={0} | all-to-all | bytes 737280 | tf_op jit(solution)/shard_map/all_to_all | solution.py:33
  242.2 14.2 %all_to_all.41 = f32[8,1,9,256]{3,1,2,0:T(1,128)S(1)} all-to-all(f32[8,1,9,256]{3,1,2,0:T(1,128)S(1)} %stack.12), channel_id=1, replica_groups=mesh['obs_0'=8,'obs_1'=4,'obs_2'=2,'rep'=4] {'obs_0'}, dimensions={0} | all-to-all | bytes 147456 | tf_op jit(solution)/shard_map/all_to_all | solution.py:15
  260.6 5.7 %all-to-all-done.4 = f32[4,8,9,256]{3,1,2,0:T(8,128)S(1)} async-done(((f32[4,8,9,256]{3,1,2,0:T(8,128)}), f32[4,8,9,256]{3,1,2,0:T(8,128)S(1)}, u32[]{:S(2)}, u32[]{:S(2)}) %all-to-all-start.4) | async-done | bytes 294944 | tf_op jit(solution)/shard_map/all_to_all | solution.py:15
  270.7 6.0 %all-to-all-done.7 = f32[4,81,256]{2,1,0:T(8,128)S(1)} async-done(((f32[4,81,256]{2,1,0:T(8,128)}), f32[4,81,256]{2,1,0:T(8,128)S(1)}, u32[]{:S(2)}, u32[]{:S(2)}) %all-to-all-start.7) | async-done | bytes 331808 | tf_op jit(solution)/shard_map/all_to_all | solution.py:68
  282.4 11.0 %all-to-all-done.5 = f32[4,32,9,256]{3,1,2,0:T(8,128)S(1)} async-done(((f32[4,32,9,256]{3,1,2,0:T(8,128)}), f32[4,32,9,256]{3,1,2,0:T(8,128)S(1)}, u32[]{:S(2)}, u32[]{:S(2)}) %all-to-all-start.5) | async-done | bytes 1179680 | tf_op jit(solution)/shard_map/all_to_all | solution.py:15
  293.8 10.7 %all_to_all.42 = f32[2,128,9,256]{3,1,2,0:T(8,128)S(1)} all-to-all(f32[2,128,9,256]{3,1,2,0:T(8,128)S(1)} %pad_maximum_fusion.1), channel_id=1, replica_groups=mesh['obs_0'=8,'obs_1'=4,'obs_2'=2,'rep'=4] {'obs_2'}, dimensions={0} | all-to-all | bytes 4718592 | tf_op jit(solution)/shard_map/all_to_all | solution.py:15
  310.1 16.8 %copy.57 = f32[9,256,256]{0,2,1:T(8,128)} copy(f32[9,256,256]{2,1,0:T(8,128)S(1)} %bitcast.49) | data formatting | bytes 4718592 | tf_op jit(solution)/shard_map/reshape | solution.py:49
  326.9 172.8 %scatter_custom_fusion = f32[9,65536]{0,1:T(8,128)} fusion(s32[65536]{0:T(1024)S(1)} %compare_select_fusion, f32[65536,9]{1,0:T(8,128)} %bitcast.45, f32[]{:T(128)} %constant.34.clone.1), kind=kCustom, calls=%fused_computation.14 | custom fusion | bytes 2359808 | tf_op jit(solution)/shard_map/scatter | solution.py:143
  499.6 19.4 %copy.56 = f32[9,65536]{1,0:T(8,128)} copy(f32[9,65536]{0,1:T(8,128)} %scatter_custom_fusion) | data formatting | bytes 4718592
  (247 shorter events, 109.9 us)
Async XLA Ops:
  3.2 24.8 %all-to-all-start.1 = ((s32[1,64,513]{2,0,1:T(1,128)}), s32[1,64,513]{2,0,1:T(1,128)S(1)}, u32[]{:S(2)}, u32[]{:S(2)}) async-start(s32[1,64,513]{2,0,1:T(1,128)} %copy.48), calls=%async_computation.1 | async-start | bytes 327680 | tf_op jit(solution)/shard_map/all_to_all | solution.py:21
  28.0 7.0 %copy-start = (s32[1,64,513]{2,0,1:T(1,128)}, s32[1,64,513]{2,0,1:T(1,128)S(1)}, u32[]{:S(2)}) copy-start(s32[1,64,513]{2,0,1:T(1,128)S(1)} %all-to-all-done.1) | copy-start | bytes 393988
  28.0 79.4 %all-to-all-start = ((f32[20,64,512]{2,0,1:T(8,128)}), f32[20,64,512]{2,0,1:T(8,128)S(1)}, u32[]{:S(2)}, u32[]{:S(2)}) async-start(f32[20,64,512]{2,0,1:T(8,128)} %copy.45), calls=%async_computation | async-start | bytes 6291456 | tf_op jit(solution)/shard_map/all_to_all | solution.py:21
  109.1 3.6 slice-start
  112.8 2.1 copy-start.1
  120.2 2.1 copy-start.1
  127.5 2.1 copy-start.1
  134.9 2.1 copy-start.1
  142.3 2.1 copy-start.1
  149.7 2.1 copy-start.1
  157.0 2.1 copy-start.1
  164.4 2.1 copy-start.1
  171.8 2.1 copy-start.1
  179.2 2.1 copy-start.1
  186.5 2.1 copy-start.1
  193.9 2.1 copy-start.1
  201.3 2.1 copy-start.1
  208.7 2.1 copy-start.1
  216.1 2.1 copy-start.1
  223.4 2.1 copy-start.1
  257.2 9.1 %all-to-all-start.4 = ((f32[4,8,9,256]{3,1,2,0:T(8,128)}), f32[4,8,9,256]{3,1,2,0:T(8,128)S(1)}, u32[]{:S(2)}, u32[]{:S(2)}) async-start(f32[4,8,9,256]{3,1,2,0:T(8,128)} %stack.13), calls=%async_computation.4 | async-start | bytes 589824 | tf_op jit(solution)/shard_map/all_to_all | solution.py:15
  267.1 14.3 %copy-start.4 = (s32[65536]{0:T(1024)S(1)}, s32[65536]{0:T(1024)}, u32[]{:S(2)}) copy-start(s32[65536]{0:T(1024)} %param.11) | copy-start | bytes 786436
  267.1 9.6 %all-to-all-start.7 = ((f32[4,81,256]{2,1,0:T(8,128)}), f32[4,81,256]{2,1,0:T(8,128)S(1)}, u32[]{:S(2)}, u32[]{:S(2)}) async-start(f32[4,81,256]{2,1,0:T(8,128)} %broadcast_in_dim.36), calls=%async_computation.7 | async-start | bytes 720896 | tf_op jit(solution)/shard_map/all_to_all | solution.py:68
  277.8 15.6 %all-to-all-start.5 = ((f32[4,32,9,256]{3,1,2,0:T(8,128)}), f32[4,32,9,256]{3,1,2,0:T(8,128)S(1)}, u32[]{:S(2)}, u32[]{:S(2)}) async-start(f32[4,32,9,256]{3,1,2,0:T(8,128)} %stack.14), calls=%async_computation.5 | async-start | bytes 2359296 | tf_op jit(solution)/shard_map/all_to_all | solution.py:15
  (17 other events, 12.8 us)
